TPU v7x, 32 devices: a whole 2x2x4 slice. The times are simulated.
32 devices in a mesh: dp: 16 (over z, y, x), mp: 2 (over core).
Axes of the slice: x: 2, y: 2, z: 4, core: 2. Of those that a mesh axis runs over, the one named last changes fastest.
Arguments:
- clean: float32 [64, 3, 4096], P(('dp', 'mp')), may hold values from -1 to 1
- noise: float32 [64, 3, 4096], P(('dp', 'mp')), may hold values from -12 to 12
- lowres: float32 [64, 3, 4096], P(('dp', 'mp')), may hold values from -1 to 1
- aug_noise: float32 [64, 3, 4096], P(('dp', 'mp')), may hold values from -5 to 5
- timesteps: int32 [64], P(('dp', 'mp')), may hold values from 0 to 999
- aug_levels: int32 [64], P(('dp', 'mp')), may hold values from 0 to 999
- lengths: int32 [64], P(('dp', 'mp')), may hold values from 1 to 128
- text: bfloat16 [64, 128, 4096], P(('dp', 'mp')), may hold values from -160 to 160
- w_stem: float32 [6, 128], replicated, may hold values from -2.5 to 2.5
- w_time: float32 [256, 256], replicated, may hold values from -0.375 to 0.375
- conv_one: bfloat16 [1152, 128], replicated, may hold values from -0.1875 to 0.1875
- conv_two: bfloat16 [1152, 128], replicated, may hold values from -0.1875 to 0.1875
- kv_weight: bfloat16 [4096, 256], P('mp'), may hold values from -0.09375 to 0.09375
- w_query: bfloat16 [128, 128], replicated, may hold values from -0.5 to 0.5
- w_output: bfloat16 [128, 128], replicated, may hold values from -0.5 to 0.5
- w_head: bfloat16 [3, 128], replicated, may hold values from -0.5 to 0.5
Outputs:
- conv_one_update: float32 [1152, 128], P(('dp', 'mp'))
- conv_two_update: float32 [1152, 128], P(('dp', 'mp'))
- kv_update: float32 [4096, 256], P('mp', 'dp')
- loss_mean: float32 [], replicated
All inputs are finite; a program needn't handle non-finite values.
Results may differ from a plain program's by a relative error of at most 0.03.
The roundings to bfloat16 on the way count: a program that leaves them out, or rounds other values in their place, can miss the bound.
Values may be sent and summed in bfloat16 or wider, within the bound.
No kernel may reach another device: no remote copies, remote signals or barrier semaphores. Data moves between devices by JAX's collectives and lax.ppermute only.
A program may use at most 128 MiB of HBM per device.

v0:
```python
import math
import jax
import jax.numpy as jnp
from jax import lax
from jax.sharding import PartitionSpec as P

S = 64
GROUPS = 32
HEADS = 2
HEAD_DIM = 64
FREQS = 64
STEPS = 1000


def signal_level(index):
    ratio = (index.astype(jnp.float32) / STEPS + 0.008) / 1.008
    cosine = jnp.cos(ratio * (math.pi / 2.0))
    return cosine * cosine


def sinusoid(index):
    freqs = jnp.exp(-math.log(10000.0) * jnp.arange(FREQS, dtype=jnp.float32) / FREQS)
    angles = index.astype(jnp.float32) * freqs
    return jnp.concatenate([jnp.sin(angles), jnp.cos(angles)])


def prepare(clean, noise, lowres, aug_noise, tstep, level, w_stem, w_time):
    signal = signal_level(tstep)
    aug_signal = signal_level(level)
    noisy = jnp.sqrt(signal) * clean + jnp.sqrt(1.0 - signal) * noise
    low_noisy = jnp.sqrt(aug_signal) * lowres + jnp.sqrt(1.0 - aug_signal) * aug_noise
    stacked = jnp.concatenate([noisy, low_noisy], axis=0)
    h_start = jnp.einsum("kp,kc->pc", stacked, w_stem, precision=lax.Precision.HIGHEST)
    feature = jnp.concatenate([sinusoid(tstep), sinusoid(level)])[None, :]
    embed = jax.nn.silu(jnp.dot(feature, w_time, precision=lax.Precision.HIGHEST))[0]
    channels = w_stem.shape[1]
    return (h_start, embed[:channels], embed[channels:])


def group_matrix(channels):
    members = channels // GROUPS
    labels = jnp.arange(channels) // members
    return (labels[:, None] == labels[None, :]).astype(jnp.float32) / members


def group_norm(values, grouping):
    average = jnp.dot(
        jnp.mean(values, axis=0, keepdims=True), grouping, precision=lax.Precision.HIGHEST
    )
    centred = values - average
    spread = jnp.dot(
        jnp.mean(centred * centred, axis=0, keepdims=True),
        grouping,
        precision=lax.Precision.HIGHEST,
    )
    return centred * lax.rsqrt(spread + 1e-05)


def convolve(activation, weight):
    channels = weight.shape[1]
    kernel = weight.reshape(3, 3, channels, channels)
    picture = activation.reshape(1, S, S, channels)
    result = lax.conv_general_dilated(
        picture,
        kernel,
        (1, 1),
        "SAME",
        dimension_numbers=("NHWC", "HWIO", "NHWC"),
        preferred_element_type=jnp.float32,
    )
    return result.reshape(S * S, channels)


def image_loss(
    conv_one, conv_two, keys_values, h_start, scale, shift, keep, w_query, w_output, w_head, noise
):
    channels = conv_one.shape[1]
    grouping = group_matrix(channels)
    act_one = jax.nn.silu(group_norm(h_start, grouping)).astype(jnp.bfloat16)
    conv_out_one = convolve(act_one, conv_one)
    act_two = jax.nn.silu(group_norm(conv_out_one, grouping) * (1.0 + scale) + shift).astype(
        jnp.bfloat16
    )
    h_mid = h_start + convolve(act_two, conv_two)
    normed = group_norm(h_mid, grouping).astype(jnp.bfloat16)
    queries = (
        jnp.dot(normed, w_query, preferred_element_type=jnp.float32) * HEAD_DIM ** (-0.5)
    ).astype(jnp.bfloat16)
    width = w_query.shape[1]
    pieces = []
    for head_index in range(HEADS):
        lower = head_index * HEAD_DIM
        upper = lower + HEAD_DIM
        scores = jnp.dot(
            queries[:, lower:upper],
            keys_values[:, lower:upper].T,
            preferred_element_type=jnp.float32,
        )
        scores = jnp.where(keep[None, :], scores, -1e30)
        highest = jnp.max(scores, axis=1, keepdims=True)
        weights = jnp.exp(scores - highest)
        probs = (weights / jnp.sum(weights, axis=1, keepdims=True)).astype(jnp.bfloat16)
        pieces.append(
            jnp.dot(
                probs,
                keys_values[:, width + lower : width + upper],
                preferred_element_type=jnp.float32,
            )
        )
    attended = jnp.concatenate(pieces, axis=1).astype(jnp.bfloat16)
    h_out = h_mid + jnp.dot(attended, w_output, preferred_element_type=jnp.float32)
    pred = jnp.einsum(
        "kc,pc->kp", w_head, h_out.astype(jnp.bfloat16), preferred_element_type=jnp.float32
    )
    error = pred - noise
    return jnp.sum(error * error)


def local(
    clean,
    noise,
    lowres,
    aug_noise,
    timesteps,
    aug_levels,
    lengths,
    text,
    w_stem,
    w_time,
    conv_one,
    conv_two,
    kv_weight,
    w_query,
    w_output,
    w_head,
):
    images = clean.shape[0]
    tokens = text.shape[1]
    features = text.shape[2]
    width = kv_weight.shape[1]
    half = kv_weight.shape[0]
    piece = lax.all_gather(kv_weight, "mp", axis=0, tiled=True)
    flat = jnp.dot(
        text.reshape(images * tokens, piece.shape[0]), piece, preferred_element_type=jnp.float32
    )
    summed = flat.reshape(images, tokens, width)
    keys_values = summed.astype(jnp.bfloat16)

    def one_image(items):
        clean_i, noise_i, low_i, aug_i, tstep, level, length, pairs = items
        h_start, scale, shift = prepare(
            clean_i, noise_i, low_i, aug_i, tstep, level, w_stem, w_time
        )
        keep = jnp.arange(tokens) < length
        value, pullback = jax.vjp(
            lambda first, second, third: image_loss(
                first,
                second,
                third,
                h_start,
                scale,
                shift,
                keep,
                w_query,
                w_output,
                w_head,
                noise_i,
            ),
            conv_one,
            conv_two,
            pairs,
        )
        part_one, part_two, part_kv = pullback(jnp.ones((), jnp.float32))
        return (part_one, part_two, part_kv, value)

    parts_one, parts_two, parts_kv, values = lax.map(
        one_image, (clean, noise, lowres, aug_noise, timesteps, aug_levels, lengths, keys_values)
    )
    local_one = jnp.sum(parts_one.astype(jnp.float32), axis=0)
    local_two = jnp.sum(parts_two.astype(jnp.float32), axis=0)
    local_loss = jnp.sum(values)
    loss_total = lax.psum(local_loss, ("dp", "mp"))
    grad_one, grad_two = (
        lax.psum_scatter(local_one, ("dp", "mp"), scatter_dimension=0, tiled=True),
        lax.psum_scatter(local_two, ("dp", "mp"), scatter_dimension=0, tiled=True),
    )
    full_grad = lax.dot_general(
        text.reshape(-1, features),
        parts_kv.reshape(-1, width),
        (((0,), (0,)), ((), ())),
        preferred_element_type=jnp.float32,
    )
    row_share = lax.psum_scatter(full_grad, "mp", scatter_dimension=0, tiled=True)
    grad_kv = lax.psum_scatter(row_share, "dp", scatter_dimension=1, tiled=True)
    square_one = jnp.sum(grad_one * grad_one)
    square_two = jnp.sum(grad_two * grad_two)
    square_kv = jnp.sum(grad_kv * grad_kv)
    total_one, total_two, total_kv = lax.psum((square_one, square_two, square_kv), ("dp", "mp"))
    conv_count = conv_one.shape[0] * conv_one.shape[1]
    kv_count = half * lax.axis_size("mp") * width
    conv_one_update = grad_one * lax.rsqrt(total_one / conv_count + 1e-06)
    conv_two_update = grad_two * lax.rsqrt(total_two / conv_count + 1e-06)
    kv_update = grad_kv * lax.rsqrt(total_kv / kv_count + 1e-06)
    loss_mean = loss_total / (
        images * lax.axis_size(("dp", "mp")) * clean.shape[1] * clean.shape[2]
    )
    return (conv_one_update, conv_two_update, kv_update, loss_mean)


def solution(mesh):
    return jax.shard_map(
        local,
        mesh=mesh,
        in_specs=(
            P(("dp", "mp"), None, None),
            P(("dp", "mp"), None, None),
            P(("dp", "mp"), None, None),
            P(("dp", "mp"), None, None),
            P(("dp", "mp")),
            P(("dp", "mp")),
            P(("dp", "mp")),
            P(("dp", "mp"), None, None),
            P(),
            P(),
            P(),
            P(),
            P("mp", None),
            P(),
            P(),
            P(),
        ),
        out_specs=(P(("dp", "mp"), None), P(("dp", "mp"), None), P("mp", "dp"), P()),
        check_vma=False,
    )
```

profile of v0, /device:TPU:0, one launch (start us, length us, event | category | flops | bytes accessed | tf_op | source)
XLA Modules:
  0.0 415.6 jit_solution(3835564456848357906)
XLA Ops:
  8.1 14.8 %all-gather.2.cloned.1.call-done = bf16[4096,256]{1,0:T(8,128)(2,1)} async-done(((bf16[2048,256]{1,0:T(8,128)(2,1)}), bf16[4096,256]{1,0:T(8,128)(2,1)}) %all-gather.2.cloned.1.call-update) | async-done | bytes 2097168 | tf_op jit(solution)/shard_map/all_gather | solution.py:142
  22.9 2.9 fusion.285
  25.8 184.8 %while.19 = (s32[]{:T(128)}, bf16[2,1152,128]{2,1,0:T(8,128)(2,1)}, bf16[2,1152,128]{2,1,0:T(8,128)(2,1)}, bf16[2,128,256]{1,2,0:T(8,128)(2,1)}, f32[2]{0:T(128)...) while((s32[]{:T(128)}, bf16[2,1152,128]{2,1,0:T(8,128)(2,1)}, ...), condition=%wide.region_22.23_spmd, body=%wide.region_0.22_spmd.sunk | while | flops 8245876736 | bytes 325935616 | solution.py:176
  33.1 3.5 fusion.464
  40.1 3.0 select_reduce_fusion.8
  46.1 1.2 fusion.474
  48.2 3.1 fusion.476
  51.9 1.2 copy.133
  58.1 2.1 convert_reduce_fusion.7
  60.2 1.1 convolution_convert_fusion.20
  62.2 2.1 convert_reduce_fusion.6
  65.4 1.2 convolution_convert_fusion.19
  66.6 3.9 multiply_reduce_fusion.17
  70.5 1.5 convolution_convert_fusion.21
  72.0 1.4 convolution_convert_fusion.22
  82.2 1.5 multiply_reduce_fusion.20
  88.3 5.1 %select_reduce_fusion.10 = (f32[128]{0:T(128)S(1)}, f32[64,8,9,128]{3,1,2,0:T(8,128)S(1)}) fusion(f32[64,8,9,128]{3,1,2,0:T(8,128)S(1)} %copy-done.8, f32[128]{0:T(128)S(1)} %copy-done.40, pred[8,9]{0,1:T(8,128)(4,1)} %get-tuple-element.839, f32[128]{0:T(128)S(1)} %copy-done.48, f32[128]{0:T(128)S(1)} %copy-done.46, f32[128]{0:T(128)S(1)} %copy-done.50, ...), kind=kOutput, calls=%fused_computation.51.clone.1 | convolution fusion | flops 1360920448 | bytes 6425160 | tf_op jit(solution)/shard_map/while/body/eval_jaxpr/transpose(jvp())/conv_general_dilated | solution.py:63
  93.6 1.4 select_reduce_fusion.11
  98.4 5.0 %fusion.499 = bf16[3,3,128,128,1]{3,2,1,4,0:T(8,128)(2,1)S(1)} fusion(bf16[64,8,9,128,1]{3,1,4,2,0:T(8,128)(2,1)S(1)} %fusion.495, bf16[64,8,9,128,1]{3,1,4,2,0:T(8,128)(2,1)S(1)} %copy.137, bf16[64,8,9,128,1]{3,1,4,2,0:T(8,128)(2,1)S(1)} %fusion.496, f32[128]{0:T(128)S(1)} %fusion.498, pred[8,9]{0,1:T(8,128)(4,1)} %get-tuple-element.839, ...), kind=kOutput, calls=%fused_computation.101.clone.1 | convolution fusion | flops 1360281600 | bytes 8554568 | tf_op jit(solution)/shard_map/while/body/eval_jaxpr/transpose(jvp())/conv_general_dilated | solution.py:63
  103.4 1.8 fusion.491
  106.5 4.8 %fusion.492 = bf16[3,3,128,128,1]{3,2,1,4,0:T(8,128)(2,1)S(1)} fusion(bf16[64,8,9,128,1]{3,0,2,1,4:T(8,128)(2,1)S(1)} %bitcast.331, bf16[64,8,9,128,1]{3,1,2,0,4:T(8,128)(2,1)S(1)} %maximum_bitcast_fusion.8, bf16[64,8,9,128,1]{3,1,2,0,4:T(8,128)(2,1)S(1)} %fusion.491, bf16[64,8,9,128,1]{3,1,2,0,4:T(8,128)(2,1)S(1)} %maximum_bitcast_fusion.9), kind=kOutput, calls=%fused_computation.100.clone.1 | convolution fusion | flops 1348337664 | bytes 5013504 | tf_op jit(solution)/shard_map/while/body/eval_jaxpr/transpose(jvp())/conv_general_dilated | solution.py:63
  123.4 3.5 fusion.464
  130.5 3.0 select_reduce_fusion.8
  136.4 1.4 fusion.474
  138.7 3.1 fusion.476
  142.5 1.2 copy.133
  148.6 2.1 convert_reduce_fusion.7
  152.8 2.1 convert_reduce_fusion.6
  155.9 1.2 convolution_convert_fusion.19
  157.2 3.9 multiply_reduce_fusion.17
  161.1 1.5 convolution_convert_fusion.21
  162.6 1.4 convolution_convert_fusion.22
  172.8 1.5 multiply_reduce_fusion.20
  178.9 4.9 %select_reduce_fusion.10 = (f32[128]{0:T(128)S(1)}, f32[64,8,9,128]{3,1,2,0:T(8,128)S(1)}) fusion(f32[64,8,9,128]{3,1,2,0:T(8,128)S(1)} %copy-done.8, f32[128]{0:T(128)S(1)} %copy-done.40, pred[8,9]{0,1:T(8,128)(4,1)} %get-tuple-element.839, f32[128]{0:T(128)S(1)} %copy-done.48, f32[128]{0:T(128)S(1)} %copy-done.46, f32[128]{0:T(128)S(1)} %copy-done.50, ...), kind=kOutput, calls=%fused_computation.51.clone.1 | convolution fusion | flops 1360920448 | bytes 6425160 | tf_op jit(solution)/shard_map/while/body/eval_jaxpr/transpose(jvp())/conv_general_dilated | solution.py:63
  184.0 1.4 select_reduce_fusion.11
  188.8 5.0 %fusion.499 = bf16[3,3,128,128,1]{3,2,1,4,0:T(8,128)(2,1)S(1)} fusion(bf16[64,8,9,128,1]{3,1,4,2,0:T(8,128)(2,1)S(1)} %fusion.495, bf16[64,8,9,128,1]{3,1,4,2,0:T(8,128)(2,1)S(1)} %copy.137, bf16[64,8,9,128,1]{3,1,4,2,0:T(8,128)(2,1)S(1)} %fusion.496, f32[128]{0:T(128)S(1)} %fusion.498, pred[8,9]{0,1:T(8,128)(4,1)} %get-tuple-element.839, ...), kind=kOutput, calls=%fused_computation.101.clone.1 | convolution fusion | flops 1360281600 | bytes 8554568 | tf_op jit(solution)/shard_map/while/body/eval_jaxpr/transpose(jvp())/conv_general_dilated | solution.py:63
  193.8 1.8 fusion.491
  196.8 5.0 %fusion.492 = bf16[3,3,128,128,1]{3,2,1,4,0:T(8,128)(2,1)S(1)} fusion(bf16[64,8,9,128,1]{3,0,2,1,4:T(8,128)(2,1)S(1)} %bitcast.331, bf16[64,8,9,128,1]{3,1,2,0,4:T(8,128)(2,1)S(1)} %maximum_bitcast_fusion.8, bf16[64,8,9,128,1]{3,1,2,0,4:T(8,128)(2,1)S(1)} %fusion.491, bf16[64,8,9,128,1]{3,1,2,0,4:T(8,128)(2,1)S(1)} %maximum_bitcast_fusion.9), kind=kOutput, calls=%fused_computation.100.clone.1 | convolution fusion | flops 1348337664 | bytes 5013504 | tf_op jit(solution)/shard_map/while/body/eval_jaxpr/transpose(jvp())/conv_general_dilated | solution.py:63
  210.7 3.6 convolution_bitcast_fusion.11
  214.4 13.2 %reduce-scatter.7.cloned.1.call-done = f32[2048,256]{0,1:T(8,128)} async-done(((f32[4096,256]{0,1:T(8,128)}), f32[2048,256]{0,1:T(8,128)}) %reduce-scatter.7.cloned.1.call-update) | async-done | bytes 2097168 | tf_op jit(solution)/shard_map/reduce_scatter | solution.py:193
  227.6 1.5 convert_reduce_fusion.2
  229.2 86.5 %fusion.288 = (f32[48,128]{1,0:T(8,128)S(1)}, f32[48,128]{1,0:T(8,128)S(1)}) fusion(f32[1152,128]{1,0:T(8,128)S(1)} %get-tuple-element.470, f32[1152,128]{1,0:T(8,128)S(1)} %get-tuple-element.469), kind=kCustom, calls=%all-reduce-scatter.2 | all-reduce-scatter fusion | flops 393217 | bytes 1228800
  315.7 1.3 collective-permute-start.15
  317.0 1.3 collective-permute-start.10
  318.3 1.3 collective-permute-start.11
  319.6 1.3 collective-permute-start.12
  320.9 1.3 collective-permute-start.13
  322.2 7.0 %collective-permute-start.7 = (f32[36,128]{1,0:T(8,128)S(1)}, f32[36,128]{1,0:T(8,128)S(1)}, u32[]{:S(2)}, u32[]{:S(2)}) collective-permute-start(f32[36,128]{1,0:T(8,128)S(1)} %slice.90), channel_id=1, source_target_pairs={{0,8},{1,9},{2,10},{3,11},{4,12},{5,13},{6,14},{7,15},{8,16},{9,17... | collective-permute-start | bytes 55304
  329.2 1.5 collective-permute-done.7
  330.7 1.3 collective-permute-start.14
  332.0 4.9 %collective-permute-start.8 = (f32[48,128]{1,0:T(8,128)S(1)}, f32[48,128]{1,0:T(8,128)S(1)}, u32[]{:S(2)}, u32[]{:S(2)}) collective-permute-start(f32[48,128]{1,0:T(8,128)S(1)} %get-tuple-element.418), channel_id=1, source_target_pairs={{0,1},{1,2},{2,3},{3,4},{4,5},{5,6},{6,7},{7,8},{8,9},{9,10},{10,1... | collective-permute-start | bytes 73736
  336.9 2.8 collective-permute-start.9
  339.7 2.6 collective-permute-start
  342.3 3.2 collective-permute-start.1
  345.5 2.9 collective-permute-start.2
  348.5 2.4 collective-permute-start.3
  350.9 2.0 collective-permute-start.4
  352.9 3.0 collective-permute-start.5
  355.9 1.6 collective-permute-start.6
  358.2 1.2 concatenate.34
  359.4 1.2 concatenate.33
  361.9 1.5 multiply_reduce_fusion.6
  363.5 38.8 %all-reduce.10 = (f32[]{:T(128)}, f32[]{:T(128)}, f32[]{:T(128)}, f32[]{:T(128)}) all-reduce(f32[]{:T(128)} %multiply_reduce_fusion.8, f32[]{:T(128)} %multiply_reduce_fusion.7, f32[]{:T(128)} %multiply_reduce_fusion.6, f32[]{:T(128)} %reduce_sum.338), channel_id=1, replica_groups=mesh['dp'=16,'mp'=2] {'dp','mp'}, use_global_device_ids=true, to_apply=%region_26.27 | all-reduce | flops 4 | bytes 32 | tf_op jit(solution)/shard_map/psum | solution.py:198
  406.2 1.6 broadcast_multiply_fusion
  (474 shorter events, 82.6 us)
Async XLA Ops:
  7.2 15.7 %copy-start = (bf16[2,128,4096]{2,1,0:T(8,128)(2,1)S(1)}, bf16[2,128,4096]{2,1,0:T(8,128)(2,1)}, u32[]{:S(2)}) copy-start(bf16[2,128,4096]{2,1,0:T(8,128)(2,1)} %param.25) | copy-start | bytes 6291460
  7.2 15.7 %all-gather.2.cloned.1.call-start = ((), (), s32[]{:S(2)}) async-start(), calls=%async_computation.2 | async-start | bytes 3145728 | tf_op jit(solution)/shard_map/all_gather | solution.py:142
  7.9 219.7 %reduce-scatter.7.cloned.1.call-start = ((), (), s32[]{:S(2)}) async-start(), calls=%async_computation.3 | async-start | bytes 6291456 | tf_op jit(solution)/shard_map/reduce_scatter | solution.py:193
  8.0 17.8 %copy-start.26 = (bf16[128,128]{1,0:T(8,128)(2,1)S(1)}, bf16[128,128]{1,0:T(8,128)(2,1)}, u32[]{:S(2)}) copy-start(bf16[128,128]{1,0:T(8,128)(2,1)} %param.31) | copy-start | bytes 98308
  8.0 17.8 %copy-start.30 = (pred[8,9]{0,1:T(8,128)(4,1)S(1)}, pred[8,9]{0,1:T(8,128)(4,1)}, u32[]{:S(2)}) copy-start(pred[8,9]{0,1:T(8,128)(4,1)} %constant.595) | copy-start | bytes 220
  8.0 17.8 %copy-start.53 = (f32[6,128]{1,0:T(8,128)S(1)}, f32[6,128]{1,0:T(8,128)}, u32[]{:S(2)}) copy-start(f32[6,128]{1,0:T(8,128)} %param.26) | copy-start | bytes 9220
  8.0 17.8 %copy-start.58 = (s32[2]{0:T(128)S(1)}, s32[2]{0:T(128)}, u32[]{:S(2)}) copy-start(s32[2]{0:T(128)} %param.22) | copy-start | bytes 28
  8.0 17.8 %copy-start.60 = (s32[2]{0:T(128)S(1)}, s32[2]{0:T(128)}, u32[]{:S(2)}) copy-start(s32[2]{0:T(128)} %param.23) | copy-start | bytes 28
  8.1 17.8 %copy-start.62 = (s32[2]{0:T(128)S(1)}, s32[2]{0:T(128)}, u32[]{:S(2)}) copy-start(s32[2]{0:T(128)} %param.24) | copy-start | bytes 28
  36.5 18.0 %copy-start.67 = (s32[128]{0:T(128)}, s32[128]{0:T(128)S(1)}, u32[]{:S(2)}) copy-start(s32[128]{0:T(128)S(1)} %and_select_fusion.2) | copy-start | bytes 1540 | tf_op jit(solution)/shard_map/while
  43.2 4.1 copy-start.7
  47.3 4.0 copy-start.9
  55.9 5.5 %copy-start.15 = (bf16[4096,128]{0,1:T(8,128)(2,1)}, bf16[4096,128]{0,1:T(8,128)(2,1)S(1)}, u32[]{:S(2)}) copy-start(bf16[4096,128]{0,1:T(8,128)(2,1)S(1)} %fusion.479) | copy-start | bytes 3145732 | tf_op jit(solution)/shard_map/while
  57.3 4.1 copy-start.41
  58.1 3.3 copy-start.21
  62.2 4.4 %copy-start.23 = (f32[4096]{0:T(1024)}, f32[4096]{0:T(1024)S(1)}, u32[]{:S(2)}) copy-start(f32[4096]{0:T(1024)S(1)} %fusion.481) | copy-start | bytes 49156 | tf_op jit(solution)/shard_map/while
  70.5 3.0 copy-start.24
  70.5 3.0 copy-start.6
  88.3 5.1 %copy-start.69 = (f32[128]{0:T(128)S(1)}, f32[128]{0:T(128)}, u32[]{:S(2)}) copy-start(f32[128]{0:T(128)} %get-tuple-element.687) | copy-start | bytes 1540 | tf_op jit(solution)/shard_map/while
  106.3 4.9 %copy-start.33 = (bf16[2,1152,128]{2,1,0:T(8,128)(2,1)S(1)}, bf16[2,1152,128]{2,1,0:T(8,128)(2,1)}, u32[]{:S(2)}) copy-start(bf16[2,1152,128]{2,1,0:T(8,128)(2,1)} %get-tuple-element.720) | copy-start | bytes 1769476 | tf_op jit(solution)/shard_map/while
  106.4 4.9 %copy-start.35 = (bf16[2,1152,128]{2,1,0:T(8,128)(2,1)S(1)}, bf16[2,1152,128]{2,1,0:T(8,128)(2,1)}, u32[]{:S(2)}) copy-start(bf16[2,1152,128]{2,1,0:T(8,128)(2,1)} %get-tuple-element.721) | copy-start | bytes 1769476 | tf_op jit(solution)/shard_map/while
  106.4 5.0 %copy-start.64 = (f32[2]{0:T(128)S(1)}, f32[2]{0:T(128)}, u32[]{:S(2)}) copy-start(f32[2]{0:T(128)} %get-tuple-element.723) | copy-start | bytes 28 | tf_op jit(solution)/shard_map/while
  106.4 6.3 %copy-start.27 = (bf16[128,128]{1,0:T(8,128)(2,1)S(1)}, bf16[128,128]{1,0:T(8,128)(2,1)}, u32[]{:S(2)}) copy-start(bf16[128,128]{1,0:T(8,128)(2,1)} %get-tuple-element.805) | copy-start | bytes 98308 | tf_op jit(solution)/shard_map/while
  106.4 6.3 %copy-start.31 = (pred[8,9]{0,1:T(8,128)(4,1)S(1)}, pred[8,9]{0,1:T(8,128)(4,1)}, u32[]{:S(2)}) copy-start(pred[8,9]{0,1:T(8,128)(4,1)} %get-tuple-element.839) | copy-start | bytes 220 | tf_op jit(solution)/shard_map/while
  106.4 6.2 %copy-start.54 = (f32[6,128]{1,0:T(8,128)S(1)}, f32[6,128]{1,0:T(8,128)}, u32[]{:S(2)}) copy-start(f32[6,128]{1,0:T(8,128)} %get-tuple-element.884) | copy-start | bytes 9220 | tf_op jit(solution)/shard_map/while
  106.4 6.2 %copy-start.59 = (s32[2]{0:T(128)S(1)}, s32[2]{0:T(128)}, u32[]{:S(2)}) copy-start(s32[2]{0:T(128)} %get-tuple-element.934) | copy-start | bytes 28 | tf_op jit(solution)/shard_map/while
  106.4 6.2 %copy-start.61 = (s32[2]{0:T(128)S(1)}, s32[2]{0:T(128)}, u32[]{:S(2)}) copy-start(s32[2]{0:T(128)} %get-tuple-element.966) | copy-start | bytes 28 | tf_op jit(solution)/shard_map/while
  106.4 6.2 %copy-start.63 = (s32[2]{0:T(128)S(1)}, s32[2]{0:T(128)}, u32[]{:S(2)}) copy-start(s32[2]{0:T(128)} %get-tuple-element.999) | copy-start | bytes 28 | tf_op jit(solution)/shard_map/while
  126.9 18.2 %copy-start.67 = (s32[128]{0:T(128)}, s32[128]{0:T(128)S(1)}, u32[]{:S(2)}) copy-start(s32[128]{0:T(128)S(1)} %and_select_fusion.2) | copy-start | bytes 1540 | tf_op jit(solution)/shard_map/while
  133.5 4.3 %copy-start.7 = (f32[64,8,9,128]{3,1,2,0:T(8,128)}, f32[64,8,9,128]{3,1,2,0:T(8,128)S(1)}, u32[]{:S(2)}) copy-start(f32[64,8,9,128]{3,1,2,0:T(8,128)S(1)} %get-tuple-element.647) | copy-start | bytes 7077892 | tf_op jit(solution)/shard_map/while
  137.8 4.0 copy-start.9
  146.5 5.5 %copy-start.15 = (bf16[4096,128]{0,1:T(8,128)(2,1)}, bf16[4096,128]{0,1:T(8,128)(2,1)S(1)}, u32[]{:S(2)}) copy-start(bf16[4096,128]{0,1:T(8,128)(2,1)S(1)} %fusion.479) | copy-start | bytes 3145732 | tf_op jit(solution)/shard_map/while
  147.9 4.1 copy-start.41
  148.6 3.3 copy-start.21
  152.8 4.4 %copy-start.23 = (f32[4096]{0:T(1024)}, f32[4096]{0:T(1024)S(1)}, u32[]{:S(2)}) copy-start(f32[4096]{0:T(1024)S(1)} %fusion.481) | copy-start | bytes 49156 | tf_op jit(solution)/shard_map/while
  161.1 3.0 copy-start.6
  178.9 4.9 %copy-start.69 = (f32[128]{0:T(128)S(1)}, f32[128]{0:T(128)}, u32[]{:S(2)}) copy-start(f32[128]{0:T(128)} %get-tuple-element.687) | copy-start | bytes 1540 | tf_op jit(solution)/shard_map/while
  196.7 5.1 %copy-start.33 = (bf16[2,1152,128]{2,1,0:T(8,128)(2,1)S(1)}, bf16[2,1152,128]{2,1,0:T(8,128)(2,1)}, u32[]{:S(2)}) copy-start(bf16[2,1152,128]{2,1,0:T(8,128)(2,1)} %get-tuple-element.720) | copy-start | bytes 1769476 | tf_op jit(solution)/shard_map/while
  196.7 5.1 %copy-start.35 = (bf16[2,1152,128]{2,1,0:T(8,128)(2,1)S(1)}, bf16[2,1152,128]{2,1,0:T(8,128)(2,1)}, u32[]{:S(2)}) copy-start(bf16[2,1152,128]{2,1,0:T(8,128)(2,1)} %get-tuple-element.721) | copy-start | bytes 1769476 | tf_op jit(solution)/shard_map/while
  196.7 5.2 %copy-start.64 = (f32[2]{0:T(128)S(1)}, f32[2]{0:T(128)}, u32[]{:S(2)}) copy-start(f32[2]{0:T(128)} %get-tuple-element.723) | copy-start | bytes 28 | tf_op jit(solution)/shard_map/while
  196.7 6.5 %copy-start.27 = (bf16[128,128]{1,0:T(8,128)(2,1)S(1)}, bf16[128,128]{1,0:T(8,128)(2,1)}, u32[]{:S(2)}) copy-start(bf16[128,128]{1,0:T(8,128)(2,1)} %get-tuple-element.805) | copy-start | bytes 98308 | tf_op jit(solution)/shard_map/while
  196.8 6.5 %copy-start.31 = (pred[8,9]{0,1:T(8,128)(4,1)S(1)}, pred[8,9]{0,1:T(8,128)(4,1)}, u32[]{:S(2)}) copy-start(pred[8,9]{0,1:T(8,128)(4,1)} %get-tuple-element.839) | copy-start | bytes 220 | tf_op jit(solution)/shard_map/while
  196.8 6.5 %copy-start.54 = (f32[6,128]{1,0:T(8,128)S(1)}, f32[6,128]{1,0:T(8,128)}, u32[]{:S(2)}) copy-start(f32[6,128]{1,0:T(8,128)} %get-tuple-element.884) | copy-start | bytes 9220 | tf_op jit(solution)/shard_map/while
  196.8 6.5 %copy-start.59 = (s32[2]{0:T(128)S(1)}, s32[2]{0:T(128)}, u32[]{:S(2)}) copy-start(s32[2]{0:T(128)} %get-tuple-element.934) | copy-start | bytes 28 | tf_op jit(solution)/shard_map/while
  196.8 6.5 %copy-start.61 = (s32[2]{0:T(128)S(1)}, s32[2]{0:T(128)}, u32[]{:S(2)}) copy-start(s32[2]{0:T(128)} %get-tuple-element.966) | copy-start | bytes 28 | tf_op jit(solution)/shard_map/while
  196.8 6.5 %copy-start.63 = (s32[2]{0:T(128)S(1)}, s32[2]{0:T(128)}, u32[]{:S(2)}) copy-start(s32[2]{0:T(128)} %get-tuple-element.999) | copy-start | bytes 28 | tf_op jit(solution)/shard_map/while
  214.3 147.6 %reduce-scatter.9.cloned.1.call-start = ((), (), s32[]{:S(2)}) async-start(), calls=%async_computation.4 | async-start | bytes 2228224 | tf_op jit(solution)/shard_map/reduce_scatter | solution.py:194
  227.6 130.0 %copy-start.66 = (f32[2]{0:T(128)S(1)}, f32[2]{0:T(128)}, u32[]{:S(2)}) copy-start(f32[2]{0:T(128)} %get-tuple-element.971) | copy-start | bytes 28
  315.7 6.5 %collective-permute-start.15 = (f32[36,128]{1,0:T(8,128)S(1)}, f32[36,128]{1,0:T(8,128)S(1)}, u32[]{:S(2)}, u32[]{:S(2)}) collective-permute-start(f32[36,128]{1,0:T(8,128)S(1)} %slice.91), channel_id=1, source_target_pairs={{0,8},{1,9},{2,10},{3,11},{4,12},{5,13},{6,14},{7,15},{8,16},{9,17... | collective-permute-start | bytes 55304
  317.0 15.0 %collective-permute-start.10 = (f32[48,128]{1,0:T(8,128)S(1)}, f32[48,128]{1,0:T(8,128)S(1)}, u32[]{:S(2)}, u32[]{:S(2)}) collective-permute-start(f32[48,128]{1,0:T(8,128)S(1)} %get-tuple-element.418), channel_id=1, source_target_pairs={{0,3},{1,4},{2,5},{3,6},{4,7},{5,8},{6,9},{7,10},{8,11},{9,12},{10... | collective-permute-start | bytes 73736
  318.3 18.7 %collective-permute-start.11 = (f32[48,128]{1,0:T(8,128)S(1)}, f32[48,128]{1,0:T(8,128)S(1)}, u32[]{:S(2)}, u32[]{:S(2)}) collective-permute-start(f32[48,128]{1,0:T(8,128)S(1)} %get-tuple-element.418), channel_id=1, source_target_pairs={{0,4},{1,5},{2,6},{3,7},{4,8},{5,9},{6,10},{7,11},{8,12},{9,13},{1... | collective-permute-start | bytes 73736
  319.6 20.1 %collective-permute-start.12 = (f32[48,128]{1,0:T(8,128)S(1)}, f32[48,128]{1,0:T(8,128)S(1)}, u32[]{:S(2)}, u32[]{:S(2)}) collective-permute-start(f32[48,128]{1,0:T(8,128)S(1)} %get-tuple-element.418), channel_id=1, source_target_pairs={{0,5},{1,6},{2,7},{3,8},{4,9},{5,10},{6,11},{7,12},{8,13},{9,14},{... | collective-permute-start | bytes 73736
  320.9 21.4 %collective-permute-start.13 = (f32[48,128]{1,0:T(8,128)S(1)}, f32[48,128]{1,0:T(8,128)S(1)}, u32[]{:S(2)}, u32[]{:S(2)}) collective-permute-start(f32[48,128]{1,0:T(8,128)S(1)} %get-tuple-element.418), channel_id=1, source_target_pairs={{0,6},{1,7},{2,8},{3,9},{4,10},{5,11},{6,12},{7,13},{8,14},{9,15},... | collective-permute-start | bytes 73736
  322.2 8.5 %collective-permute-start.7 = (f32[36,128]{1,0:T(8,128)S(1)}, f32[36,128]{1,0:T(8,128)S(1)}, u32[]{:S(2)}, u32[]{:S(2)}) collective-permute-start(f32[36,128]{1,0:T(8,128)S(1)} %slice.90), channel_id=1, source_target_pairs={{0,8},{1,9},{2,10},{3,11},{4,12},{5,13},{6,14},{7,15},{8,16},{9,17... | collective-permute-start | bytes 55304
  330.7 14.8 %collective-permute-start.14 = (f32[48,128]{1,0:T(8,128)S(1)}, f32[48,128]{1,0:T(8,128)S(1)}, u32[]{:S(2)}, u32[]{:S(2)}) collective-permute-start(f32[48,128]{1,0:T(8,128)S(1)} %get-tuple-element.418), channel_id=1, source_target_pairs={{0,7},{1,8},{2,9},{3,10},{4,11},{5,12},{6,13},{7,14},{8,15},{9,16}... | collective-permute-start | bytes 73736
  332.0 16.5 %collective-permute-start.8 = (f32[48,128]{1,0:T(8,128)S(1)}, f32[48,128]{1,0:T(8,128)S(1)}, u32[]{:S(2)}, u32[]{:S(2)}) collective-permute-start(f32[48,128]{1,0:T(8,128)S(1)} %get-tuple-element.418), channel_id=1, source_target_pairs={{0,1},{1,2},{2,3},{3,4},{4,5},{5,6},{6,7},{7,8},{8,9},{9,10},{10,1... | collective-permute-start | bytes 73736
  336.9 14.0 %collective-permute-start.9 = (f32[48,128]{1,0:T(8,128)S(1)}, f32[48,128]{1,0:T(8,128)S(1)}, u32[]{:S(2)}, u32[]{:S(2)}) collective-permute-start(f32[48,128]{1,0:T(8,128)S(1)} %get-tuple-element.418), channel_id=1, source_target_pairs={{0,2},{1,3},{2,4},{3,5},{4,6},{5,7},{6,8},{7,9},{8,10},{9,11},{10,... | collective-permute-start | bytes 73736
  339.7 13.2 %collective-permute-start = (f32[48,128]{1,0:T(8,128)S(1)}, f32[48,128]{1,0:T(8,128)S(1)}, u32[]{:S(2)}, u32[]{:S(2)}) collective-permute-start(f32[48,128]{1,0:T(8,128)S(1)} %get-tuple-element.417), channel_id=1, source_target_pairs={{0,1},{1,2},{2,3},{3,4},{4,5},{5,6},{6,7},{7,8},{8,9},{9,10},{10,1... | collective-permute-start | bytes 73736
  342.3 13.6 %collective-permute-start.1 = (f32[48,128]{1,0:T(8,128)S(1)}, f32[48,128]{1,0:T(8,128)S(1)}, u32[]{:S(2)}, u32[]{:S(2)}) collective-permute-start(f32[48,128]{1,0:T(8,128)S(1)} %get-tuple-element.417), channel_id=1, source_target_pairs={{0,2},{1,3},{2,4},{3,5},{4,6},{5,7},{6,8},{7,9},{8,10},{9,11},{10,... | collective-permute-start | bytes 73736
  345.5 13.9 %collective-permute-start.2 = (f32[48,128]{1,0:T(8,128)S(1)}, f32[48,128]{1,0:T(8,128)S(1)}, u32[]{:S(2)}, u32[]{:S(2)}) collective-permute-start(f32[48,128]{1,0:T(8,128)S(1)} %get-tuple-element.417), channel_id=1, source_target_pairs={{0,3},{1,4},{2,5},{3,6},{4,7},{5,8},{6,9},{7,10},{8,11},{9,12},{10... | collective-permute-start | bytes 73736
  348.5 10.9 %collective-permute-start.3 = (f32[48,128]{1,0:T(8,128)S(1)}, f32[48,128]{1,0:T(8,128)S(1)}, u32[]{:S(2)}, u32[]{:S(2)}) collective-permute-start(f32[48,128]{1,0:T(8,128)S(1)} %get-tuple-element.417), channel_id=1, source_target_pairs={{0,4},{1,5},{2,6},{3,7},{4,8},{5,9},{6,10},{7,11},{8,12},{9,13},{1... | collective-permute-start | bytes 73736
  350.9 8.5 %collective-permute-start.4 = (f32[48,128]{1,0:T(8,128)S(1)}, f32[48,128]{1,0:T(8,128)S(1)}, u32[]{:S(2)}, u32[]{:S(2)}) collective-permute-start(f32[48,128]{1,0:T(8,128)S(1)} %get-tuple-element.417), channel_id=1, source_target_pairs={{0,5},{1,6},{2,7},{3,8},{4,9},{5,10},{6,11},{7,12},{8,13},{9,14},{... | collective-permute-start | bytes 73736
  352.9 6.5 %collective-permute-start.5 = (f32[48,128]{1,0:T(8,128)S(1)}, f32[48,128]{1,0:T(8,128)S(1)}, u32[]{:S(2)}, u32[]{:S(2)}) collective-permute-start(f32[48,128]{1,0:T(8,128)S(1)} %get-tuple-element.417), channel_id=1, source_target_pairs={{0,6},{1,7},{2,8},{3,9},{4,10},{5,11},{6,12},{7,13},{8,14},{9,15},... | collective-permute-start | bytes 73736
  355.9 3.5 collective-permute-start.6
  (89 other events, 125.2 us)
Sparse Core Ops, SparseCore 0:
  9.5 13.2 all-gather.1
  214.4 13.0 reduce-scatter.6
  229.9 82.9 reduce-scatter.8
where the time goes:
time: 419 us; the launch traced here: 416 us
  blocking collectives  125 us (30%)
  matrix products  95.9 us (23%)
  local copies, waits for them, and re-layouts  48.1 us (11%)
  other arithmetic  40.4 us (10%)
  starting transfers between devices  40.3 us (10%)
  waiting for transfers between devices  30.2 us (7%)
  between operations  18.3 us (4%)
  loops' own time  17.2 us (4%)
    unnamed x1, blocking collectives  86.5 us
    conv_general_dilated x10, matrix products, convolve(): lax.conv_general_dilated(picture, kernel, (1, 1), 'SAME', dimension_numbe...  41.9 us
    unnamed x16, starting transfers between devices  40.2 us
    psum x1, blocking collectives, local(): lax.psum((square_one, square_two, square_kv), ('dp', 'mp'))  38.8 us
    while x260, local copies, waits for them, and re-layouts  17.9 us
    another operation x1, loops' own time, local(): lax.map(one_image, (clean, noise, lowres, aug_noise, timesteps, aug_level...  17.2 us
    all_gather x1, waiting for transfers between devices, local(): piece = lax.all_gather(kv_weight, 'mp', axis=0, tiled=True)  14.8 us
    reduce_scatter x1, waiting for transfers between devices, local(): lax.psum_scatter(full_grad, 'mp', scatter_dimension=0, tiled=True)  13.2 us
  transfers between devices with their start and end apart: 19, of which 3 were waited for; matrix products, arithmetic and copies ran while one was open for 22% of the time, Pallas kernels for 0%

commit v1 on v0

--- a/solution.py
+++ b/solution.py
@@ -195,7 +195,9 @@
     square_one = jnp.sum(grad_one * grad_one)
     square_two = jnp.sum(grad_two * grad_two)
     square_kv = jnp.sum(grad_kv * grad_kv)
-    total_one, total_two, total_kv = lax.psum((square_one, square_two, square_kv), ("dp", "mp"))
+    total_one, total_two, total_kv = lax.psum(
+        lax.psum((square_one, square_two, square_kv), "mp"), "dp"
+    )
     conv_count = conv_one.shape[0] * conv_one.shape[1]
     kv_count = half * lax.axis_size("mp") * width
     conv_one_update = grad_one * lax.rsqrt(total_one / conv_count + 1e-06)

time: 419 us -> 463 us (1.11)
  blocking collectives: 125 us -> 169 us
    psum x1 -> x3, blocking collectives: 38.8 us -> 81.4 us  [the longest x1 41.1 us: local(): lax.psum(lax.psum((square_one, square_two, square_kv), 'mp'), 'dp')]
  transfers between devices with their start and end apart: 19 -> 19, of which waited for: 3 -> 3; matrix products, arithmetic and copies ran while one was open for 22% -> 20% of each run, Pallas kernels for 0% -> 0%
where the time goes in v1:
time: 463 us; the launch traced here: 460 us
  blocking collectives  169 us (37%)
  matrix products  95.9 us (21%)
  local copies, waits for them, and re-layouts  48.2 us (10%)
  other arithmetic  40.4 us (9%)
  starting transfers between devices  40.3 us (9%)
  waiting for transfers between devices  30.2 us (7%)
  between operations  18.2 us (4%)
  loops' own time  17.2 us (4%)
    unnamed x1, blocking collectives  87.8 us
    conv_general_dilated x10, matrix products, convolve(): lax.conv_general_dilated(picture, kernel, (1, 1), 'SAME', dimension_numbe...  41.9 us
    psum x1, blocking collectives, local(): lax.psum(lax.psum((square_one, square_two, square_kv), 'mp'), 'dp')  41.1 us
    unnamed x16, starting transfers between devices  40.2 us
    psum x1, blocking collectives, local(): loss_total = lax.psum(local_loss, ('dp', 'mp'))  37.2 us
    while x260, local copies, waits for them, and re-layouts  17.9 us
    another operation x1, loops' own time, local(): lax.map(one_image, (clean, noise, lowres, aug_noise, timesteps, aug_level...  17.2 us
    all_gather x1, waiting for transfers between devices, local(): piece = lax.all_gather(kv_weight, 'mp', axis=0, tiled=True)  14.8 us
  transfers between devices with their start and end apart: 19, of which 3 were waited for; matrix products, arithmetic and copies ran while one was open for 20% of the time, Pallas kernels for 0%

profile of v1, /device:TPU:0, one launch (start us, length us, event | category | flops | bytes accessed | tf_op | source)
XLA Modules:
  0.0 459.7 jit_solution(2932644069435206900)
XLA Ops:
  8.1 14.8 %all-gather.2.cloned.1.call-done = bf16[4096,256]{1,0:T(8,128)(2,1)} async-done(((bf16[2048,256]{1,0:T(8,128)(2,1)}), bf16[4096,256]{1,0:T(8,128)(2,1)}) %all-gather.2.cloned.1.call-update) | async-done | bytes 2097168 | tf_op jit(solution)/shard_map/all_gather | solution.py:142
  22.9 3.0 fusion.285
  25.9 184.9 %while.19 = (s32[]{:T(128)}, bf16[2,1152,128]{2,1,0:T(8,128)(2,1)}, bf16[2,1152,128]{2,1,0:T(8,128)(2,1)}, bf16[2,128,256]{1,2,0:T(8,128)(2,1)}, f32[2]{0:T(128)...) while((s32[]{:T(128)}, bf16[2,1152,128]{2,1,0:T(8,128)(2,1)}, ...), condition=%wide.region_22.23_spmd, body=%wide.region_0.22_spmd.sunk | while | flops 8245876736 | bytes 325935616 | solution.py:176
  33.1 3.5 fusion.464
  40.2 3.0 select_reduce_fusion.8
  48.2 3.1 fusion.476
  52.0 1.2 copy.133
  58.1 2.1 convert_reduce_fusion.7
  62.2 2.1 convert_reduce_fusion.6
  65.4 1.2 convolution_convert_fusion.19
  66.6 3.9 multiply_reduce_fusion.17
  70.5 1.5 convolution_convert_fusion.21
  72.1 1.4 convolution_convert_fusion.22
  82.3 1.5 multiply_reduce_fusion.20
  88.4 5.1 %select_reduce_fusion.10 = (f32[128]{0:T(128)S(1)}, f32[64,8,9,128]{3,1,2,0:T(8,128)S(1)}) fusion(f32[64,8,9,128]{3,1,2,0:T(8,128)S(1)} %copy-done.8, f32[128]{0:T(128)S(1)} %copy-done.40, pred[8,9]{0,1:T(8,128)(4,1)} %get-tuple-element.841, f32[128]{0:T(128)S(1)} %copy-done.48, f32[128]{0:T(128)S(1)} %copy-done.46, f32[128]{0:T(128)S(1)} %copy-done.50, ...), kind=kOutput, calls=%fused_computation.51.clone.1 | convolution fusion | flops 1360920448 | bytes 6425160 | tf_op jit(solution)/shard_map/while/body/eval_jaxpr/transpose(jvp())/conv_general_dilated | solution.py:63
  93.7 1.4 select_reduce_fusion.11
  98.5 5.0 %fusion.499 = bf16[3,3,128,128,1]{3,2,1,4,0:T(8,128)(2,1)S(1)} fusion(bf16[64,8,9,128,1]{3,1,4,2,0:T(8,128)(2,1)S(1)} %fusion.495, bf16[64,8,9,128,1]{3,1,4,2,0:T(8,128)(2,1)S(1)} %copy.137, bf16[64,8,9,128,1]{3,1,4,2,0:T(8,128)(2,1)S(1)} %fusion.496, f32[128]{0:T(128)S(1)} %fusion.498, pred[8,9]{0,1:T(8,128)(4,1)} %get-tuple-element.841, ...), kind=kOutput, calls=%fused_computation.101.clone.1 | convolution fusion | flops 1360281600 | bytes 8554568 | tf_op jit(solution)/shard_map/while/body/eval_jaxpr/transpose(jvp())/conv_general_dilated | solution.py:63
  103.5 1.8 fusion.491
  106.5 4.8 %fusion.492 = bf16[3,3,128,128,1]{3,2,1,4,0:T(8,128)(2,1)S(1)} fusion(bf16[64,8,9,128,1]{3,0,2,1,4:T(8,128)(2,1)S(1)} %bitcast.331, bf16[64,8,9,128,1]{3,1,2,0,4:T(8,128)(2,1)S(1)} %maximum_bitcast_fusion.8, bf16[64,8,9,128,1]{3,1,2,0,4:T(8,128)(2,1)S(1)} %fusion.491, bf16[64,8,9,128,1]{3,1,2,0,4:T(8,128)(2,1)S(1)} %maximum_bitcast_fusion.9), kind=kOutput, calls=%fused_computation.100.clone.1 | convolution fusion | flops 1348337664 | bytes 5013504 | tf_op jit(solution)/shard_map/while/body/eval_jaxpr/transpose(jvp())/conv_general_dilated | solution.py:63
  123.4 3.5 fusion.464
  130.5 3.0 select_reduce_fusion.8
  136.5 1.4 fusion.474
  138.8 3.1 fusion.476
  142.6 1.2 copy.133
  148.6 2.1 convert_reduce_fusion.7
  152.8 2.1 convert_reduce_fusion.6
  155.9 1.2 convolution_convert_fusion.19
  157.2 3.9 multiply_reduce_fusion.17
  161.1 1.5 convolution_convert_fusion.21
  162.6 1.4 convolution_convert_fusion.22
  172.8 1.5 multiply_reduce_fusion.20
  178.9 4.9 %select_reduce_fusion.10 = (f32[128]{0:T(128)S(1)}, f32[64,8,9,128]{3,1,2,0:T(8,128)S(1)}) fusion(f32[64,8,9,128]{3,1,2,0:T(8,128)S(1)} %copy-done.8, f32[128]{0:T(128)S(1)} %copy-done.40, pred[8,9]{0,1:T(8,128)(4,1)} %get-tuple-element.841, f32[128]{0:T(128)S(1)} %copy-done.48, f32[128]{0:T(128)S(1)} %copy-done.46, f32[128]{0:T(128)S(1)} %copy-done.50, ...), kind=kOutput, calls=%fused_computation.51.clone.1 | convolution fusion | flops 1360920448 | bytes 6425160 | tf_op jit(solution)/shard_map/while/body/eval_jaxpr/transpose(jvp())/conv_general_dilated | solution.py:63
  184.0 1.4 select_reduce_fusion.11
  188.8 5.0 %fusion.499 = bf16[3,3,128,128,1]{3,2,1,4,0:T(8,128)(2,1)S(1)} fusion(bf16[64,8,9,128,1]{3,1,4,2,0:T(8,128)(2,1)S(1)} %fusion.495, bf16[64,8,9,128,1]{3,1,4,2,0:T(8,128)(2,1)S(1)} %copy.137, bf16[64,8,9,128,1]{3,1,4,2,0:T(8,128)(2,1)S(1)} %fusion.496, f32[128]{0:T(128)S(1)} %fusion.498, pred[8,9]{0,1:T(8,128)(4,1)} %get-tuple-element.841, ...), kind=kOutput, calls=%fused_computation.101.clone.1 | convolution fusion | flops 1360281600 | bytes 8554568 | tf_op jit(solution)/shard_map/while/body/eval_jaxpr/transpose(jvp())/conv_general_dilated | solution.py:63
  193.8 1.8 fusion.491
  196.8 5.0 %fusion.492 = bf16[3,3,128,128,1]{3,2,1,4,0:T(8,128)(2,1)S(1)} fusion(bf16[64,8,9,128,1]{3,0,2,1,4:T(8,128)(2,1)S(1)} %bitcast.331, bf16[64,8,9,128,1]{3,1,2,0,4:T(8,128)(2,1)S(1)} %maximum_bitcast_fusion.8, bf16[64,8,9,128,1]{3,1,2,0,4:T(8,128)(2,1)S(1)} %fusion.491, bf16[64,8,9,128,1]{3,1,2,0,4:T(8,128)(2,1)S(1)} %maximum_bitcast_fusion.9), kind=kOutput, calls=%fused_computation.100.clone.1 | convolution fusion | flops 1348337664 | bytes 5013504 | tf_op jit(solution)/shard_map/while/body/eval_jaxpr/transpose(jvp())/conv_general_dilated | solution.py:63
  210.8 3.6 convolution_bitcast_fusion.11
  214.5 13.2 %reduce-scatter.7.cloned.1.call-done = f32[2048,256]{0,1:T(8,128)} async-done(((f32[4096,256]{0,1:T(8,128)}), f32[2048,256]{0,1:T(8,128)}) %reduce-scatter.7.cloned.1.call-update) | async-done | bytes 2097168 | tf_op jit(solution)/shard_map/reduce_scatter | solution.py:193
  227.7 1.5 convert_reduce_fusion.2
  229.3 87.8 %fusion.288 = (f32[48,128]{1,0:T(8,128)S(1)}, f32[48,128]{1,0:T(8,128)S(1)}) fusion(f32[1152,128]{1,0:T(8,128)S(1)} %get-tuple-element.472, f32[1152,128]{1,0:T(8,128)S(1)} %get-tuple-element.471), kind=kCustom, calls=%all-reduce-scatter.2 | all-reduce-scatter fusion | flops 393217 | bytes 1228800
  317.1 1.3 collective-permute-start.15
  318.4 1.3 collective-permute-start.10
  319.7 1.3 collective-permute-start.11
  321.0 1.3 collective-permute-start.12
  322.3 1.3 collective-permute-start.13
  323.6 7.0 %collective-permute-start.7 = (f32[36,128]{1,0:T(8,128)S(1)}, f32[36,128]{1,0:T(8,128)S(1)}, u32[]{:S(2)}, u32[]{:S(2)}) collective-permute-start(f32[36,128]{1,0:T(8,128)S(1)} %slice.90), channel_id=1, source_target_pairs={{0,8},{1,9},{2,10},{3,11},{4,12},{5,13},{6,14},{7,15},{8,16},{9,17... | collective-permute-start | bytes 55304
  330.7 1.5 collective-permute-done.7
  332.1 1.3 collective-permute-start.14
  333.4 4.9 %collective-permute-start.8 = (f32[48,128]{1,0:T(8,128)S(1)}, f32[48,128]{1,0:T(8,128)S(1)}, u32[]{:S(2)}, u32[]{:S(2)}) collective-permute-start(f32[48,128]{1,0:T(8,128)S(1)} %get-tuple-element.420), channel_id=1, source_target_pairs={{0,1},{1,2},{2,3},{3,4},{4,5},{5,6},{6,7},{7,8},{8,9},{9,10},{10,1... | collective-permute-start | bytes 73736
  338.4 2.8 collective-permute-start.9
  341.1 2.6 collective-permute-start
  343.7 3.2 collective-permute-start.1
  347.0 2.9 collective-permute-start.2
  349.9 2.4 collective-permute-start.3
  352.3 2.0 collective-permute-start.4
  354.4 3.0 collective-permute-start.5
  357.4 1.6 collective-permute-start.6
  359.6 37.2 %psum.55 = f32[]{:T(128)} all-reduce(f32[]{:T(128)} %reduce_sum.338), channel_id=1, replica_groups=mesh['dp'=16,'mp'=2] {'dp','mp'}, use_global_device_ids=true, to_apply=%region_39.40 | all-reduce | flops 1 | bytes 8 | tf_op jit(solution)/shard_map/psum | solution.py:182
  396.8 1.2 concatenate.34
  398.1 1.2 concatenate.33
  400.5 1.5 multiply_reduce_fusion.6
  402.7 3.1 all-reduce.11
  405.8 41.1 %all-reduce.10 = (f32[]{:T(128)}, f32[]{:T(128)}, f32[]{:T(128)}) all-reduce(f32[]{:T(128)} %get-tuple-element.414, f32[]{:T(128)} %get-tuple-element.415, f32[]{:T(128)} %get-tuple-element.416), channel_id=1, replica_groups=mesh['dp'=16,'mp'=2] {'dp'}, use_global_device_ids=true, to_apply=%region_27.28 | all-reduce | flops 3 | bytes 24 | tf_op jit(solution)/shard_map/psum | solution.py:198
  450.3 1.6 broadcast_multiply_fusion
  (476 shorter events, 85.0 us)
Async XLA Ops:
  7.2 15.7 %copy-start = (bf16[2,128,4096]{2,1,0:T(8,128)(2,1)S(1)}, bf16[2,128,4096]{2,1,0:T(8,128)(2,1)}, u32[]{:S(2)}) copy-start(bf16[2,128,4096]{2,1,0:T(8,128)(2,1)} %param.25) | copy-start | bytes 6291460
  7.2 15.7 %all-gather.2.cloned.1.call-start = ((), (), s32[]{:S(2)}) async-start(), calls=%async_computation.2 | async-start | bytes 3145728 | tf_op jit(solution)/shard_map/all_gather | solution.py:142
  7.9 219.8 %reduce-scatter.7.cloned.1.call-start = ((), (), s32[]{:S(2)}) async-start(), calls=%async_computation.3 | async-start | bytes 6291456 | tf_op jit(solution)/shard_map/reduce_scatter | solution.py:193
  8.0 17.8 %copy-start.26 = (bf16[128,128]{1,0:T(8,128)(2,1)S(1)}, bf16[128,128]{1,0:T(8,128)(2,1)}, u32[]{:S(2)}) copy-start(bf16[128,128]{1,0:T(8,128)(2,1)} %param.31) | copy-start | bytes 98308
  8.0 17.8 %copy-start.30 = (pred[8,9]{0,1:T(8,128)(4,1)S(1)}, pred[8,9]{0,1:T(8,128)(4,1)}, u32[]{:S(2)}) copy-start(pred[8,9]{0,1:T(8,128)(4,1)} %constant.595) | copy-start | bytes 220
  8.0 17.8 %copy-start.53 = (f32[6,128]{1,0:T(8,128)S(1)}, f32[6,128]{1,0:T(8,128)}, u32[]{:S(2)}) copy-start(f32[6,128]{1,0:T(8,128)} %param.26) | copy-start | bytes 9220
  8.0 17.8 %copy-start.58 = (s32[2]{0:T(128)S(1)}, s32[2]{0:T(128)}, u32[]{:S(2)}) copy-start(s32[2]{0:T(128)} %param.22) | copy-start | bytes 28
  8.0 17.8 %copy-start.60 = (s32[2]{0:T(128)S(1)}, s32[2]{0:T(128)}, u32[]{:S(2)}) copy-start(s32[2]{0:T(128)} %param.23) | copy-start | bytes 28
  8.1 17.8 %copy-start.62 = (s32[2]{0:T(128)S(1)}, s32[2]{0:T(128)}, u32[]{:S(2)}) copy-start(s32[2]{0:T(128)} %param.24) | copy-start | bytes 28
  36.6 18.0 %copy-start.67 = (s32[128]{0:T(128)}, s32[128]{0:T(128)S(1)}, u32[]{:S(2)}) copy-start(s32[128]{0:T(128)S(1)} %and_select_fusion.2) | copy-start | bytes 1540 | tf_op jit(solution)/shard_map/while
  43.2 4.1 copy-start.7
  47.3 4.0 copy-start.9
  55.9 5.5 %copy-start.15 = (bf16[4096,128]{0,1:T(8,128)(2,1)}, bf16[4096,128]{0,1:T(8,128)(2,1)S(1)}, u32[]{:S(2)}) copy-start(bf16[4096,128]{0,1:T(8,128)(2,1)S(1)} %fusion.479) | copy-start | bytes 3145732 | tf_op jit(solution)/shard_map/while
  57.3 4.1 copy-start.41
  58.1 3.3 copy-start.21
  62.2 4.4 copy-start.23
  70.5 3.0 copy-start.24
  70.5 3.0 copy-start.6
  88.4 5.1 %copy-start.69 = (f32[128]{0:T(128)S(1)}, f32[128]{0:T(128)}, u32[]{:S(2)}) copy-start(f32[128]{0:T(128)} %get-tuple-element.689) | copy-start | bytes 1540 | tf_op jit(solution)/shard_map/while
  106.4 4.9 %copy-start.33 = (bf16[2,1152,128]{2,1,0:T(8,128)(2,1)S(1)}, bf16[2,1152,128]{2,1,0:T(8,128)(2,1)}, u32[]{:S(2)}) copy-start(bf16[2,1152,128]{2,1,0:T(8,128)(2,1)} %get-tuple-element.722) | copy-start | bytes 1769476 | tf_op jit(solution)/shard_map/while
  106.4 4.9 %copy-start.35 = (bf16[2,1152,128]{2,1,0:T(8,128)(2,1)S(1)}, bf16[2,1152,128]{2,1,0:T(8,128)(2,1)}, u32[]{:S(2)}) copy-start(bf16[2,1152,128]{2,1,0:T(8,128)(2,1)} %get-tuple-element.723) | copy-start | bytes 1769476 | tf_op jit(solution)/shard_map/while
  106.4 5.0 %copy-start.64 = (f32[2]{0:T(128)S(1)}, f32[2]{0:T(128)}, u32[]{:S(2)}) copy-start(f32[2]{0:T(128)} %get-tuple-element.725) | copy-start | bytes 28 | tf_op jit(solution)/shard_map/while
  106.4 6.3 %copy-start.27 = (bf16[128,128]{1,0:T(8,128)(2,1)S(1)}, bf16[128,128]{1,0:T(8,128)(2,1)}, u32[]{:S(2)}) copy-start(bf16[128,128]{1,0:T(8,128)(2,1)} %get-tuple-element.807) | copy-start | bytes 98308 | tf_op jit(solution)/shard_map/while
  106.4 6.3 %copy-start.31 = (pred[8,9]{0,1:T(8,128)(4,1)S(1)}, pred[8,9]{0,1:T(8,128)(4,1)}, u32[]{:S(2)}) copy-start(pred[8,9]{0,1:T(8,128)(4,1)} %get-tuple-element.841) | copy-start | bytes 220 | tf_op jit(solution)/shard_map/while
  106.5 6.3 %copy-start.54 = (f32[6,128]{1,0:T(8,128)S(1)}, f32[6,128]{1,0:T(8,128)}, u32[]{:S(2)}) copy-start(f32[6,128]{1,0:T(8,128)} %get-tuple-element.886) | copy-start | bytes 9220 | tf_op jit(solution)/shard_map/while
  106.5 6.3 %copy-start.59 = (s32[2]{0:T(128)S(1)}, s32[2]{0:T(128)}, u32[]{:S(2)}) copy-start(s32[2]{0:T(128)} %get-tuple-element.936) | copy-start | bytes 28 | tf_op jit(solution)/shard_map/while
  106.5 6.3 %copy-start.61 = (s32[2]{0:T(128)S(1)}, s32[2]{0:T(128)}, u32[]{:S(2)}) copy-start(s32[2]{0:T(128)} %get-tuple-element.968) | copy-start | bytes 28 | tf_op jit(solution)/shard_map/while
  106.5 6.3 %copy-start.63 = (s32[2]{0:T(128)S(1)}, s32[2]{0:T(128)}, u32[]{:S(2)}) copy-start(s32[2]{0:T(128)} %get-tuple-element.1001) | copy-start | bytes 28 | tf_op jit(solution)/shard_map/while
  126.9 18.2 %copy-start.67 = (s32[128]{0:T(128)}, s32[128]{0:T(128)S(1)}, u32[]{:S(2)}) copy-start(s32[128]{0:T(128)S(1)} %and_select_fusion.2) | copy-start | bytes 1540 | tf_op jit(solution)/shard_map/while
  133.5 4.3 copy-start.7
  137.9 4.0 copy-start.9
  146.5 5.5 %copy-start.15 = (bf16[4096,128]{0,1:T(8,128)(2,1)}, bf16[4096,128]{0,1:T(8,128)(2,1)S(1)}, u32[]{:S(2)}) copy-start(bf16[4096,128]{0,1:T(8,128)(2,1)S(1)} %fusion.479) | copy-start | bytes 3145732 | tf_op jit(solution)/shard_map/while
  147.9 4.1 copy-start.41
  148.6 3.3 copy-start.21
  152.8 4.4 copy-start.23
  161.1 3.0 copy-start.6
  178.9 4.9 %copy-start.69 = (f32[128]{0:T(128)S(1)}, f32[128]{0:T(128)}, u32[]{:S(2)}) copy-start(f32[128]{0:T(128)} %get-tuple-element.689) | copy-start | bytes 1540 | tf_op jit(solution)/shard_map/while
  196.7 5.1 %copy-start.33 = (bf16[2,1152,128]{2,1,0:T(8,128)(2,1)S(1)}, bf16[2,1152,128]{2,1,0:T(8,128)(2,1)}, u32[]{:S(2)}) copy-start(bf16[2,1152,128]{2,1,0:T(8,128)(2,1)} %get-tuple-element.722) | copy-start | bytes 1769476 | tf_op jit(solution)/shard_map/while
  196.7 5.1 %copy-start.35 = (bf16[2,1152,128]{2,1,0:T(8,128)(2,1)S(1)}, bf16[2,1152,128]{2,1,0:T(8,128)(2,1)}, u32[]{:S(2)}) copy-start(bf16[2,1152,128]{2,1,0:T(8,128)(2,1)} %get-tuple-element.723) | copy-start | bytes 1769476 | tf_op jit(solution)/shard_map/while
  196.8 5.2 %copy-start.64 = (f32[2]{0:T(128)S(1)}, f32[2]{0:T(128)}, u32[]{:S(2)}) copy-start(f32[2]{0:T(128)} %get-tuple-element.725) | copy-start | bytes 28 | tf_op jit(solution)/shard_map/while
  196.8 6.6 %copy-start.27 = (bf16[128,128]{1,0:T(8,128)(2,1)S(1)}, bf16[128,128]{1,0:T(8,128)(2,1)}, u32[]{:S(2)}) copy-start(bf16[128,128]{1,0:T(8,128)(2,1)} %get-tuple-element.807) | copy-start | bytes 98308 | tf_op jit(solution)/shard_map/while
  196.8 6.6 %copy-start.31 = (pred[8,9]{0,1:T(8,128)(4,1)S(1)}, pred[8,9]{0,1:T(8,128)(4,1)}, u32[]{:S(2)}) copy-start(pred[8,9]{0,1:T(8,128)(4,1)} %get-tuple-element.841) | copy-start | bytes 220 | tf_op jit(solution)/shard_map/while
  196.8 6.5 %copy-start.54 = (f32[6,128]{1,0:T(8,128)S(1)}, f32[6,128]{1,0:T(8,128)}, u32[]{:S(2)}) copy-start(f32[6,128]{1,0:T(8,128)} %get-tuple-element.886) | copy-start | bytes 9220 | tf_op jit(solution)/shard_map/while
  196.8 6.5 %copy-start.59 = (s32[2]{0:T(128)S(1)}, s32[2]{0:T(128)}, u32[]{:S(2)}) copy-start(s32[2]{0:T(128)} %get-tuple-element.936) | copy-start | bytes 28 | tf_op jit(solution)/shard_map/while
  196.8 6.5 %copy-start.61 = (s32[2]{0:T(128)S(1)}, s32[2]{0:T(128)}, u32[]{:S(2)}) copy-start(s32[2]{0:T(128)} %get-tuple-element.968) | copy-start | bytes 28 | tf_op jit(solution)/shard_map/while
  196.8 6.5 %copy-start.63 = (s32[2]{0:T(128)S(1)}, s32[2]{0:T(128)}, u32[]{:S(2)}) copy-start(s32[2]{0:T(128)} %get-tuple-element.1001) | copy-start | bytes 28 | tf_op jit(solution)/shard_map/while
  214.4 186.1 %reduce-scatter.9.cloned.1.call-start = ((), (), s32[]{:S(2)}) async-start(), calls=%async_computation.4 | async-start | bytes 2228224 | tf_op jit(solution)/shard_map/reduce_scatter | solution.py:194
  227.7 131.3 %copy-start.66 = (f32[2]{0:T(128)S(1)}, f32[2]{0:T(128)}, u32[]{:S(2)}) copy-start(f32[2]{0:T(128)} %get-tuple-element.973) | copy-start | bytes 28
  317.1 6.5 %collective-permute-start.15 = (f32[36,128]{1,0:T(8,128)S(1)}, f32[36,128]{1,0:T(8,128)S(1)}, u32[]{:S(2)}, u32[]{:S(2)}) collective-permute-start(f32[36,128]{1,0:T(8,128)S(1)} %slice.91), channel_id=1, source_target_pairs={{0,8},{1,9},{2,10},{3,11},{4,12},{5,13},{6,14},{7,15},{8,16},{9,17... | collective-permute-start | bytes 55304
  318.4 15.0 %collective-permute-start.10 = (f32[48,128]{1,0:T(8,128)S(1)}, f32[48,128]{1,0:T(8,128)S(1)}, u32[]{:S(2)}, u32[]{:S(2)}) collective-permute-start(f32[48,128]{1,0:T(8,128)S(1)} %get-tuple-element.420), channel_id=1, source_target_pairs={{0,3},{1,4},{2,5},{3,6},{4,7},{5,8},{6,9},{7,10},{8,11},{9,12},{10... | collective-permute-start | bytes 73736
  319.7 18.7 %collective-permute-start.11 = (f32[48,128]{1,0:T(8,128)S(1)}, f32[48,128]{1,0:T(8,128)S(1)}, u32[]{:S(2)}, u32[]{:S(2)}) collective-permute-start(f32[48,128]{1,0:T(8,128)S(1)} %get-tuple-element.420), channel_id=1, source_target_pairs={{0,4},{1,5},{2,6},{3,7},{4,8},{5,9},{6,10},{7,11},{8,12},{9,13},{1... | collective-permute-start | bytes 73736
  321.0 20.1 %collective-permute-start.12 = (f32[48,128]{1,0:T(8,128)S(1)}, f32[48,128]{1,0:T(8,128)S(1)}, u32[]{:S(2)}, u32[]{:S(2)}) collective-permute-start(f32[48,128]{1,0:T(8,128)S(1)} %get-tuple-element.420), channel_id=1, source_target_pairs={{0,5},{1,6},{2,7},{3,8},{4,9},{5,10},{6,11},{7,12},{8,13},{9,14},{... | collective-permute-start | bytes 73736
  322.3 21.4 %collective-permute-start.13 = (f32[48,128]{1,0:T(8,128)S(1)}, f32[48,128]{1,0:T(8,128)S(1)}, u32[]{:S(2)}, u32[]{:S(2)}) collective-permute-start(f32[48,128]{1,0:T(8,128)S(1)} %get-tuple-element.420), channel_id=1, source_target_pairs={{0,6},{1,7},{2,8},{3,9},{4,10},{5,11},{6,12},{7,13},{8,14},{9,15},... | collective-permute-start | bytes 73736
  323.6 8.5 %collective-permute-start.7 = (f32[36,128]{1,0:T(8,128)S(1)}, f32[36,128]{1,0:T(8,128)S(1)}, u32[]{:S(2)}, u32[]{:S(2)}) collective-permute-start(f32[36,128]{1,0:T(8,128)S(1)} %slice.90), channel_id=1, source_target_pairs={{0,8},{1,9},{2,10},{3,11},{4,12},{5,13},{6,14},{7,15},{8,16},{9,17... | collective-permute-start | bytes 55304
  332.1 14.8 %collective-permute-start.14 = (f32[48,128]{1,0:T(8,128)S(1)}, f32[48,128]{1,0:T(8,128)S(1)}, u32[]{:S(2)}, u32[]{:S(2)}) collective-permute-start(f32[48,128]{1,0:T(8,128)S(1)} %get-tuple-element.420), channel_id=1, source_target_pairs={{0,7},{1,8},{2,9},{3,10},{4,11},{5,12},{6,13},{7,14},{8,15},{9,16}... | collective-permute-start | bytes 73736
  333.4 16.5 %collective-permute-start.8 = (f32[48,128]{1,0:T(8,128)S(1)}, f32[48,128]{1,0:T(8,128)S(1)}, u32[]{:S(2)}, u32[]{:S(2)}) collective-permute-start(f32[48,128]{1,0:T(8,128)S(1)} %get-tuple-element.420), channel_id=1, source_target_pairs={{0,1},{1,2},{2,3},{3,4},{4,5},{5,6},{6,7},{7,8},{8,9},{9,10},{10,1... | collective-permute-start | bytes 73736
  338.4 14.0 %collective-permute-start.9 = (f32[48,128]{1,0:T(8,128)S(1)}, f32[48,128]{1,0:T(8,128)S(1)}, u32[]{:S(2)}, u32[]{:S(2)}) collective-permute-start(f32[48,128]{1,0:T(8,128)S(1)} %get-tuple-element.420), channel_id=1, source_target_pairs={{0,2},{1,3},{2,4},{3,5},{4,6},{5,7},{6,8},{7,9},{8,10},{9,11},{10,... | collective-permute-start | bytes 73736
  341.1 13.2 %collective-permute-start = (f32[48,128]{1,0:T(8,128)S(1)}, f32[48,128]{1,0:T(8,128)S(1)}, u32[]{:S(2)}, u32[]{:S(2)}) collective-permute-start(f32[48,128]{1,0:T(8,128)S(1)} %get-tuple-element.419), channel_id=1, source_target_pairs={{0,1},{1,2},{2,3},{3,4},{4,5},{5,6},{6,7},{7,8},{8,9},{9,10},{10,1... | collective-permute-start | bytes 73736
  343.7 13.6 %collective-permute-start.1 = (f32[48,128]{1,0:T(8,128)S(1)}, f32[48,128]{1,0:T(8,128)S(1)}, u32[]{:S(2)}, u32[]{:S(2)}) collective-permute-start(f32[48,128]{1,0:T(8,128)S(1)} %get-tuple-element.419), channel_id=1, source_target_pairs={{0,2},{1,3},{2,4},{3,5},{4,6},{5,7},{6,8},{7,9},{8,10},{9,11},{10,... | collective-permute-start | bytes 73736
  347.0 51.0 %collective-permute-start.2 = (f32[48,128]{1,0:T(8,128)S(1)}, f32[48,128]{1,0:T(8,128)S(1)}, u32[]{:S(2)}, u32[]{:S(2)}) collective-permute-start(f32[48,128]{1,0:T(8,128)S(1)} %get-tuple-element.419), channel_id=1, source_target_pairs={{0,3},{1,4},{2,5},{3,6},{4,7},{5,8},{6,9},{7,10},{8,11},{9,12},{10... | collective-permute-start | bytes 73736
  349.9 48.1 %collective-permute-start.3 = (f32[48,128]{1,0:T(8,128)S(1)}, f32[48,128]{1,0:T(8,128)S(1)}, u32[]{:S(2)}, u32[]{:S(2)}) collective-permute-start(f32[48,128]{1,0:T(8,128)S(1)} %get-tuple-element.419), channel_id=1, source_target_pairs={{0,4},{1,5},{2,6},{3,7},{4,8},{5,9},{6,10},{7,11},{8,12},{9,13},{1... | collective-permute-start | bytes 73736
  352.3 45.7 %collective-permute-start.4 = (f32[48,128]{1,0:T(8,128)S(1)}, f32[48,128]{1,0:T(8,128)S(1)}, u32[]{:S(2)}, u32[]{:S(2)}) collective-permute-start(f32[48,128]{1,0:T(8,128)S(1)} %get-tuple-element.419), channel_id=1, source_target_pairs={{0,5},{1,6},{2,7},{3,8},{4,9},{5,10},{6,11},{7,12},{8,13},{9,14},{... | collective-permute-start | bytes 73736
  354.4 43.7 %collective-permute-start.5 = (f32[48,128]{1,0:T(8,128)S(1)}, f32[48,128]{1,0:T(8,128)S(1)}, u32[]{:S(2)}, u32[]{:S(2)}) collective-permute-start(f32[48,128]{1,0:T(8,128)S(1)} %get-tuple-element.419), channel_id=1, source_target_pairs={{0,6},{1,7},{2,8},{3,9},{4,10},{5,11},{6,12},{7,13},{8,14},{9,15},... | collective-permute-start | bytes 73736
  357.4 40.7 %collective-permute-start.6 = (f32[48,128]{1,0:T(8,128)S(1)}, f32[48,128]{1,0:T(8,128)S(1)}, u32[]{:S(2)}, u32[]{:S(2)}) collective-permute-start(f32[48,128]{1,0:T(8,128)S(1)} %get-tuple-element.419), channel_id=1, source_target_pairs={{0,7},{1,8},{2,9},{3,10},{4,11},{5,12},{6,13},{7,14},{8,15},{9,16}... | collective-permute-start | bytes 73736
  (89 other events, 124.8 us)
Sparse Core Ops, SparseCore 0:
  9.5 13.2 all-gather.1
  214.5 13.0 reduce-scatter.6
  230.0 82.6 reduce-scatter.8
